TPU v7x, 32 devices: a whole 2x2x4 slice. The times are simulated.
32 devices in a mesh: fsdp: 4 (over z), seq: 4 (over y, x), tp: 2 (over core).
Axes of the slice: x: 2, y: 2, z: 4, core: 2. Of those that a mesh axis runs over, the one named last changes fastest.
Arguments:
- tokens: bfloat16 [4, 8, 256, 384], P(None, 'fsdp', 'seq'), may hold values from -6 to 6
- lengths: int32 [4, 8], P(None, 'fsdp'), may hold values from 64 to 256, as said below
- grad_out: bfloat16 [4, 8, 256, 384], P(None, 'fsdp', 'seq'), may hold values from -6 to 6
- qkv_weight: float32 [3, 384, 384], P(None, 'fsdp', 'tp'), may hold values from -0.3125 to 0.3125
- out_weight: float32 [384, 384], P('tp', 'fsdp'), may hold values from -1.25 to 1.25
- up_weight: float32 [384, 1536], P('fsdp', 'tp'), may hold values from -0.3125 to 0.3125
- down_weight: float32 [1536, 384], P('tp', 'fsdp'), may hold values from -0.15625 to 0.15625
- attn_gain: float32 [384], P('fsdp'), may hold values from 0.25 to 1.75
- ffn_gain: float32 [384], P('fsdp'), may hold values from 0.25 to 1.75
- moment_qkv: float32 [3, 384, 384], P(None, 'fsdp', 'tp'), may hold values from -3 to 3
- moment_out: float32 [384, 384], P('tp', 'fsdp'), may hold values from -3 to 3
- moment_up: float32 [384, 1536], P('fsdp', 'tp'), may hold values from -3 to 3
- moment_down: float32 [1536, 384], P('tp', 'fsdp'), may hold values from -3 to 3
- moment_attn: float32 [384], P('fsdp'), may hold values from -3 to 3
- moment_ffn: float32 [384], P('fsdp'), may hold values from -3 to 3
Outputs:
- block_out: bfloat16 [4, 8, 256, 384], P(None, 'fsdp', 'seq')
- input_grad: float32 [4, 8, 256, 384], P(None, 'fsdp', 'seq')
- qkv_grad: float32 [3, 384, 384], P(None, 'fsdp', 'tp')
- out_grad: float32 [384, 384], P('tp', 'fsdp')
- up_grad: float32 [384, 1536], P('fsdp', 'tp')
- down_grad: float32 [1536, 384], P('tp', 'fsdp')
- attn_gain_grad: float32 [384], P('fsdp')
- ffn_gain_grad: float32 [384], P('fsdp')
- new_qkv: float32 [3, 384, 384], P(None, 'fsdp', 'tp')
- new_out: float32 [384, 384], P('tp', 'fsdp')
- new_up: float32 [384, 1536], P('fsdp', 'tp')
- new_down: float32 [1536, 384], P('tp', 'fsdp')
- new_attn_gain: float32 [384], P('fsdp')
- new_ffn_gain: float32 [384], P('fsdp')
- new_moment_qkv: float32 [3, 384, 384], P(None, 'fsdp', 'tp')
- new_moment_out: float32 [384, 384], P('tp', 'fsdp')
- new_moment_up: float32 [384, 1536], P('fsdp', 'tp')
- new_moment_down: float32 [1536, 384], P('tp', 'fsdp')
- new_moment_attn: float32 [384], P('fsdp')
- new_moment_ffn: float32 [384], P('fsdp')
Inputs may be any that keep to these rules, and one draw needn't show every extreme that they name: `lengths`: slots at or past an image's length are padding; in every micro-batch one image has all 256 slots valid and one has 64.
All inputs are finite; a program needn't handle non-finite values.
Results may differ from a plain program's by a relative error of at most 0.012.
The roundings to bfloat16 on the way count: a program that leaves them out, or rounds other values in their place, can miss the bound.
Values may be sent and summed in bfloat16 or wider, within the bound.
A program may use at most 128 MiB of HBM per device.

v0:
```python
import math

import jax
import jax.numpy as jnp
from jax import lax
from jax.sharding import PartitionSpec as P

HEAD_DIM = 64
NS_STEPS = 5


def shortened(shard):

    def short(part):
        return part.astype(jnp.bfloat16) if part.dtype == jnp.float32 else part

    return jax.tree.map(short, shard)


def layer_stats(values):
    center = values - jnp.mean(values, axis=-1, keepdims=True)
    inv_std = lax.rsqrt(jnp.mean(center * center, axis=-1, keepdims=True) + 1e-06)
    return (center * inv_std, inv_std)


def norm_back(upstream, plain, inv_std, gain):
    scaled = upstream * gain
    return inv_std * (
        scaled
        - jnp.mean(scaled, axis=-1, keepdims=True)
        - plain * jnp.mean(scaled * plain, axis=-1, keepdims=True)
    )


def normal_cdf(values):
    return 0.5 * (1.0 + jax.scipy.special.erf(values * 0.7071067811865476))


def normal_pdf(values):
    return 0.3989422804014327 * jnp.exp(-0.5 * values * values)


def orthogonalize(matrix):
    tall = matrix.shape[0] > matrix.shape[1]
    current = matrix.T if tall else matrix
    current = current / (jnp.sqrt(jnp.sum(current * current)) + 1e-07)
    for sweep in range(NS_STEPS):
        gram = jnp.dot(current, current.T, precision=lax.Precision.HIGHEST)
        poly = -4.775 * gram + 2.0315 * jnp.dot(gram, gram, precision=lax.Precision.HIGHEST)
        current = 3.4445 * current + jnp.dot(poly, current, precision=lax.Precision.HIGHEST)
    return current.T if tall else current


def muon_delta(moment):
    ratio = math.sqrt(max(1.0, moment.shape[0] / moment.shape[1]))
    return 0.5 * ratio * orthogonalize(moment)


def owned_deltas(owner, qkv_full, out_full, up_full, down_full):
    f32 = jnp.float32
    empty = (
        jnp.zeros(qkv_full.shape, f32),
        jnp.zeros(out_full.shape, f32),
        jnp.zeros(up_full.shape, f32),
        jnp.zeros(down_full.shape, f32),
    )

    def make_qkv(which):

        def branch(unused):
            return (
                empty[0].at[which].set(muon_delta(qkv_full[which])),
                empty[1],
                empty[2],
                empty[3],
            )

        return branch

    def make_out(unused):
        return (empty[0], muon_delta(out_full), empty[2], empty[3])

    def make_up(unused):
        return (empty[0], empty[1], muon_delta(up_full), empty[3])

    def make_down(unused):
        return (empty[0], empty[1], empty[2], muon_delta(down_full))

    def make_none(unused):
        return empty

    branches = [make_qkv(0), make_qkv(1), make_qkv(2), make_out, make_up, make_down, make_none]
    return lax.switch(jnp.minimum(owner, 6), branches, 0)


def body(
    tokens,
    lengths,
    grad_out,
    qkv_weight,
    out_weight,
    up_weight,
    down_weight,
    attn_gain,
    ffn_gain,
    moment_qkv,
    moment_out,
    moment_up,
    moment_down,
    moment_attn,
    moment_ffn,
):
    f32 = jnp.float32
    bf16 = jnp.bfloat16
    micro, img_dev, tok_loc, width = tokens.shape
    seq_size = lax.axis_size("seq")
    fsdp_size = lax.axis_size("fsdp")
    tp_size = lax.axis_size("tp")
    full_len = tok_loc * seq_size
    rows = img_dev * tok_loc
    local_width = qkv_weight.shape[2]
    local_heads = local_width // HEAD_DIM
    shard_rows = qkv_weight.shape[1]
    local_ff = up_weight.shape[1]
    score_scale = HEAD_DIM ** (-0.5)
    grad_scale = (micro * img_dev * fsdp_size * full_len) ** (-0.5)

    def tp_total(partial_rows):
        return lax.psum(partial_rows, "tp")

    def head_scores(query_h, keys_all, valid):
        keys_h = keys_all.reshape(img_dev, full_len, local_heads, HEAD_DIM)
        scores = (
            jnp.einsum("iqhe,ikhe->ihqk", query_h, keys_h, preferred_element_type=f32) * score_scale
        )
        return jnp.where(valid[:, None, None, :], scores, -jnp.inf)

    sum_qkv = jnp.zeros((3, width, local_width), f32)
    sum_out = jnp.zeros((local_width, width), f32)
    sum_up = jnp.zeros((width, local_ff), f32)
    sum_down = jnp.zeros((local_ff, width), f32)
    sum_attn = jnp.zeros((width,), f32)
    sum_ffn = jnp.zeros((width,), f32)
    outputs = []
    input_grads = []
    for step in range(micro):
        gathered = (
            lax.all_gather(qkv_weight.astype(bf16), "fsdp", axis=1, tiled=True),
            lax.all_gather(out_weight.astype(bf16), "fsdp", axis=1, tiled=True),
            lax.all_gather(up_weight.astype(bf16), "fsdp", axis=0, tiled=True),
            lax.all_gather(down_weight.astype(bf16), "fsdp", axis=1, tiled=True),
            lax.all_gather(attn_gain.astype(bf16), "fsdp", axis=0, tiled=True),
            lax.all_gather(ffn_gain.astype(bf16), "fsdp", axis=0, tiled=True),
        )
        qkv_use, out_use, up_use, down_use, attn_half, ffn_half = gathered
        attn_use = attn_half.astype(f32)
        ffn_use = ffn_half.astype(f32)
        input_rows = tokens[step].reshape(rows, width).astype(f32)
        plain_attn, inv_attn = layer_stats(input_rows)
        norm_attn = (plain_attn * attn_use).astype(bf16)
        projected = jnp.einsum(
            "rd,tdh->trh", norm_attn, qkv_use, preferred_element_type=f32
        ).astype(bf16)
        query_h = projected[0].reshape(img_dev, tok_loc, local_heads, HEAD_DIM)
        keys_loc = projected[1].reshape(img_dev, tok_loc, local_width)
        values_loc = projected[2].reshape(img_dev, tok_loc, local_width)
        keys_all = lax.all_gather(keys_loc, "seq", axis=1, tiled=True)
        values_all = lax.all_gather(values_loc, "seq", axis=1, tiled=True)
        valid = lax.broadcasted_iota(jnp.int32, (img_dev, full_len), 1) < lengths[step][:, None]
        scores = head_scores(query_h, keys_all, valid)
        lse = jax.nn.logsumexp(scores, axis=-1, keepdims=True)
        probs = jnp.exp(scores - lse).astype(bf16)
        values_h = values_all.reshape(img_dev, full_len, local_heads, HEAD_DIM)
        attended = (
            jnp.einsum("ihqk,ikhe->iqhe", probs, values_h, preferred_element_type=f32)
            .astype(bf16)
            .reshape(rows, local_width)
        )
        middle = input_rows + tp_total(jnp.dot(attended, out_use, preferred_element_type=f32))
        plain_ffn, inv_ffn = layer_stats(middle)
        norm_ffn = (plain_ffn * ffn_use).astype(bf16)
        hidden = jnp.dot(norm_ffn, up_use, preferred_element_type=f32)
        activated = (hidden * normal_cdf(hidden)).astype(bf16)
        middle_out = tp_total(jnp.dot(activated, down_use, preferred_element_type=f32))
        outputs.append((middle + middle_out).astype(bf16).reshape(img_dev, tok_loc, width))
        upstream = grad_out[step].reshape(rows, width)
        back_act = jnp.einsum("rd,fd->rf", upstream, down_use, preferred_element_type=f32)
        back_hidden = (back_act * (normal_cdf(hidden) + hidden * normal_pdf(hidden))).astype(bf16)
        sum_down = sum_down + jnp.einsum(
            "rf,rd->fd", activated, upstream, preferred_element_type=f32
        )
        sum_up = sum_up + jnp.einsum("rd,rf->df", norm_ffn, back_hidden, preferred_element_type=f32)
        back_ffn = tp_total(
            jnp.einsum("rf,df->rd", back_hidden, up_use, preferred_element_type=f32)
        )
        sum_ffn = sum_ffn + jnp.sum(back_ffn * plain_ffn, axis=0)
        back_middle = upstream.astype(f32) + norm_back(back_ffn, plain_ffn, inv_ffn, ffn_use)
        middle_half = back_middle.astype(bf16)
        sum_out = sum_out + jnp.einsum(
            "rh,rd->hd", attended, middle_half, preferred_element_type=f32
        )
        back_attended = jnp.einsum(
            "rd,hd->rh", middle_half, out_use, preferred_element_type=f32
        ).astype(bf16)
        back_heads = back_attended.reshape(img_dev, tok_loc, local_heads, HEAD_DIM)
        weights = jnp.exp(head_scores(query_h, keys_all, valid) - lse)
        back_probs = jnp.einsum("iqhe,ikhe->ihqk", back_heads, values_h, preferred_element_type=f32)
        delta = jnp.sum(weights * back_probs, axis=-1, keepdims=True)
        back_scores = (weights * (back_probs - delta) * score_scale).astype(bf16)
        keys_h = keys_all.reshape(img_dev, full_len, local_heads, HEAD_DIM)
        back_query = (
            jnp.einsum("ihqk,ikhe->iqhe", back_scores, keys_h, preferred_element_type=f32)
            .astype(bf16)
            .reshape(rows, local_width)
        )
        key_part = jnp.einsum(
            "ihqk,iqhe->ikhe", back_scores, query_h, preferred_element_type=f32
        ).reshape(img_dev, full_len, local_width)
        value_part = jnp.einsum(
            "ihqk,iqhe->ikhe", probs, back_heads, preferred_element_type=f32
        ).reshape(img_dev, full_len, local_width)
        back_keys, back_values = (
            lax.psum_scatter(key_part, "seq", scatter_dimension=1, tiled=True),
            lax.psum_scatter(value_part, "seq", scatter_dimension=1, tiled=True),
        )
        back_proj = jnp.stack(
            [
                back_query,
                back_keys.astype(bf16).reshape(rows, local_width),
                back_values.astype(bf16).reshape(rows, local_width),
            ]
        )
        sum_qkv = sum_qkv + jnp.einsum(
            "rd,trh->tdh", norm_attn, back_proj, preferred_element_type=f32
        )
        back_attn = tp_total(
            jnp.einsum("trh,tdh->rd", back_proj, qkv_use, preferred_element_type=f32)
        )
        sum_attn = sum_attn + jnp.sum(back_attn * plain_attn, axis=0)
        input_rows_grad = back_middle + norm_back(back_attn, plain_attn, inv_attn, attn_use)
        input_grads.append(input_rows_grad.reshape(img_dev, tok_loc, width))
    block_out = jnp.stack(outputs)
    input_grad = jnp.stack(input_grads)
    summed = lax.psum((sum_qkv, sum_out, sum_up, sum_down, sum_attn, sum_ffn), "seq")
    shards = (
        lax.psum_scatter(summed[0], "fsdp", scatter_dimension=1, tiled=True),
        lax.psum_scatter(summed[1], "fsdp", scatter_dimension=1, tiled=True),
        lax.psum_scatter(summed[2], "fsdp", scatter_dimension=0, tiled=True),
        lax.psum_scatter(summed[3], "fsdp", scatter_dimension=1, tiled=True),
        lax.psum_scatter(summed[4], "fsdp", scatter_dimension=0, tiled=True),
        lax.psum_scatter(summed[5], "fsdp", scatter_dimension=0, tiled=True),
    )
    qkv_grad, out_grad, up_grad, down_grad, attn_gain_grad, ffn_gain_grad = tuple(
        (shard * grad_scale for shard in shards)
    )
    new_moment_qkv = 0.5 * moment_qkv + qkv_grad
    new_moment_out = 0.5 * moment_out + out_grad
    new_moment_up = 0.5 * moment_up + up_grad
    new_moment_down = 0.5 * moment_down + down_grad
    new_moment_attn = 0.5 * moment_attn + attn_gain_grad
    new_moment_ffn = 0.5 * moment_ffn + ffn_gain_grad
    moment_part = (
        lax.all_gather(new_moment_qkv, "fsdp", axis=1, tiled=True),
        lax.all_gather(new_moment_out, "fsdp", axis=1, tiled=True),
        lax.all_gather(new_moment_up, "fsdp", axis=0, tiled=True),
        lax.all_gather(new_moment_down, "fsdp", axis=1, tiled=True),
    )
    qkv_full, out_full, up_full, down_full = (
        lax.all_gather(moment_part[0], "tp", axis=2, tiled=True),
        lax.all_gather(moment_part[1], "tp", axis=0, tiled=True),
        lax.all_gather(moment_part[2], "tp", axis=1, tiled=True),
        lax.all_gather(moment_part[3], "tp", axis=0, tiled=True),
    )
    fsdp_index = lax.axis_index("fsdp")
    tp_index = lax.axis_index("tp")
    owner = fsdp_index * tp_size + tp_index
    mine = owned_deltas(owner, qkv_full, out_full, up_full, down_full)
    qkv_whole, out_whole, up_whole, down_whole = jax.tree.map(
        lambda part: part.astype(jnp.float32), lax.psum(shortened(mine), ("fsdp", "tp"))
    )
    qkv_delta = lax.dynamic_slice(
        qkv_whole,
        (0, fsdp_index * shard_rows, tp_index * local_width),
        (3, shard_rows, local_width),
    )
    out_delta = lax.dynamic_slice(
        out_whole, (tp_index * local_width, fsdp_index * shard_rows), (local_width, shard_rows)
    )
    up_delta = lax.dynamic_slice(
        up_whole, (fsdp_index * shard_rows, tp_index * local_ff), (shard_rows, local_ff)
    )
    down_delta = lax.dynamic_slice(
        down_whole, (tp_index * local_ff, fsdp_index * shard_rows), (local_ff, shard_rows)
    )
    new_qkv = qkv_weight - qkv_delta
    new_out = out_weight - out_delta
    new_up = up_weight - up_delta
    new_down = down_weight - down_delta
    new_attn_gain = attn_gain - 0.3 * new_moment_attn
    new_ffn_gain = ffn_gain - 0.3 * new_moment_ffn
    return (
        block_out,
        input_grad,
        qkv_grad,
        out_grad,
        up_grad,
        down_grad,
        attn_gain_grad,
        ffn_gain_grad,
        new_qkv,
        new_out,
        new_up,
        new_down,
        new_attn_gain,
        new_ffn_gain,
        new_moment_qkv,
        new_moment_out,
        new_moment_up,
        new_moment_down,
        new_moment_attn,
        new_moment_ffn,
    )


def solution(mesh):
    placed = (
        P(None, "fsdp", "seq", None),
        P(None, "fsdp"),
        P(None, "fsdp", "seq", None),
        P(None, "fsdp", "tp"),
        P("tp", "fsdp"),
        P("fsdp", "tp"),
        P("tp", "fsdp"),
        P("fsdp"),
        P("fsdp"),
        P(None, "fsdp", "tp"),
        P("tp", "fsdp"),
        P("fsdp", "tp"),
        P("tp", "fsdp"),
        P("fsdp"),
        P("fsdp"),
    )
    return jax.shard_map(
        body,
        mesh=mesh,
        in_specs=placed,
        out_specs=(
            P(None, "fsdp", "seq", None),
            P(None, "fsdp", "seq", None),
            P(None, "fsdp", "tp"),
            P("tp", "fsdp"),
            P("fsdp", "tp"),
            P("tp", "fsdp"),
            P("fsdp"),
            P("fsdp"),
            P(None, "fsdp", "tp"),
            P("tp", "fsdp"),
            P("fsdp", "tp"),
            P("tp", "fsdp"),
            P("fsdp"),
            P("fsdp"),
            P(None, "fsdp", "tp"),
            P("tp", "fsdp"),
            P("fsdp", "tp"),
            P("tp", "fsdp"),
            P("fsdp"),
            P("fsdp"),
        ),
        check_vma=False,
    )
```

profile of v0, /device:TPU:0, one launch (start us, length us, event | category | flops | bytes accessed | tf_op | source)
XLA Modules:
  0.0 940.1 jit_solution(8373879359125002443)
XLA Ops:
  13.9 14.0 %all-reduce.14 = (bf16[384]{0:T(512)(128)(2,1)S(1)}, bf16[384]{0:T(512)(128)(2,1)}) all-reduce(bf16[384]{0:T(512)(128)(2,1)S(1)} %dynamic-update-slice.9, bf16[384]{0:T(512)(128)(2,1)S(1)} %dynamic-update-slice.10), channel_id=1, replica_groups=mesh['fsdp'=4,'seq'=4,'tp'=2] {'fsdp'}, use_global_device_ids=true, to_apply=%add.3 | all-reduce | flops 768 | bytes 3072
  29.5 16.6 %all_gather.103 = bf16[3,384,192]{2,0,1:T(4,128)(2,1)S(1)} all-gather(bf16[3,96,192]{2,0,1:T(4,128)(2,1)S(1)} %copy.301), channel_id=1, replica_groups=mesh['fsdp'=4,'seq'=4,'tp'=2] {'fsdp'}, dimensions={1}, use_global_device_ids=true | all-gather | bytes 552960 | tf_op jit(solution)/shard_map/all_gather | solution.py:148
  47.7 9.0 all_gather.114
  57.0 9.0 all_gather.115
  68.1 13.6 %all_gather.106 = bf16[192,384]{0,1:T(8,128)(2,1)S(1)} all-gather(bf16[192,96]{0,1:T(8,128)(2,1)S(1)} %copy.309), channel_id=1, replica_groups=mesh['fsdp'=4,'seq'=4,'tp'=2] {'fsdp'}, dimensions={1}, use_global_device_ids=true | all-gather | bytes 184320 | tf_op jit(solution)/shard_map/all_gather | solution.py:149
  82.2 8.0 all_gather.112
  90.5 9.3 all_gather.113
  103.5 7.7 all_gather.110
  111.5 10.0 %all_gather.111 = bf16[2,256,192]{2,1,0:T(8,128)(2,1)S(1)} all-gather(bf16[2,64,192]{2,1,0:T(8,128)(2,1)S(1)} %bitcast.615), channel_id=1, replica_groups=mesh['fsdp'=4,'seq'=4,'tp'=2] {'seq'}, dimensions={1}, use_global_device_ids=true | all-gather | bytes 245760 | tf_op jit(solution)/shard_map/all_gather | solution.py:167
  124.9 7.5 all_gather.104
  132.7 9.6 %all_gather.105 = bf16[2,256,192]{2,1,0:T(8,128)(2,1)S(1)} all-gather(bf16[2,64,192]{2,1,0:T(8,128)(2,1)S(1)} %bitcast.617), channel_id=1, replica_groups=mesh['fsdp'=4,'seq'=4,'tp'=2] {'seq'}, dimensions={1}, use_global_device_ids=true | all-gather | bytes 245760 | tf_op jit(solution)/shard_map/all_gather | solution.py:167
  146.4 14.9 %all_gather.109 = bf16[768,384]{0,1:T(8,128)(2,1)S(1)} all-gather(bf16[768,96]{0,1:T(8,128)(2,1)S(1)} %convert_element_type.346), channel_id=1, replica_groups=mesh['fsdp'=4,'seq'=4,'tp'=2] {'fsdp'}, dimensions={1}, use_global_device_ids=true | all-gather | bytes 737280 | tf_op jit(solution)/shard_map/all_gather | solution.py:151
  161.3 15.2 %all_gather.108 = bf16[384,768]{1,0:T(8,128)(2,1)S(1)} all-gather(bf16[96,768]{1,0:T(8,128)(2,1)S(1)} %convert_element_type.344), channel_id=1, replica_groups=mesh['fsdp'=4,'seq'=4,'tp'=2] {'fsdp'}, dimensions={0}, use_global_device_ids=true | all-gather | bytes 737280 | tf_op jit(solution)/shard_map/all_gather | solution.py:150
  188.6 18.7 %all-reduce.25.cloned.1.call-done = (f32[128,384]{1,0:T(8,128)}, f32[128,384]{1,0:T(8,128)}, f32[128,384]{1,0:T(8,128)}, f32[128,384]{1,0:T(8,128)}) async-done(((f32[128,384]{1,0:T(8,128)}, f32[128,384]{1,0:T(8,128)}, f32[128,384]{1,0:T(8,128)}, f32[128,384]{1,0:T(8,128)}), (f32[128,384]{1,0:T(8,128)}, f32[128,384]{1,0:T(8,128)}, f32[128,384]{1,0:T(8,128)}, ...) | async-done | bytes 786448 | tf_op jit(solution)/shard_map/psum | solution.py:129
  304.5 26.8 %reduce-scatter.17.cloned.1.call-done = f32[2,64,192]{2,1,0:T(8,128)} async-done(((f32[2,256,192]{2,1,0:T(8,128)}), f32[2,64,192]{2,1,0:T(8,128)}) %reduce-scatter.17.cloned.1.call-update) | async-done | bytes 98320 | tf_op jit(solution)/shard_map/reduce_scatter | solution.py:223
  334.4 25.5 %reduce-scatter.31.cloned.1.call-done = f32[2,64,192]{2,1,0:T(8,128)} async-done(((f32[2,256,192]{2,1,0:T(8,128)}), f32[2,64,192]{2,1,0:T(8,128)}) %reduce-scatter.31.cloned.1.call-update) | async-done | bytes 98320 | tf_op jit(solution)/shard_map/reduce_scatter | solution.py:224
  360.9 26.9 %reduce-scatter.29.cloned.1.call-done = f32[2,64,192]{2,1,0:T(8,128)} async-done(((f32[2,256,192]{2,1,0:T(8,128)}), f32[2,64,192]{2,1,0:T(8,128)}) %reduce-scatter.29.cloned.1.call-update) | async-done | bytes 98320 | tf_op jit(solution)/shard_map/reduce_scatter | solution.py:223
  390.3 25.5 %reduce-scatter.27.cloned.1.call-done = f32[2,64,192]{2,1,0:T(8,128)} async-done(((f32[2,256,192]{2,1,0:T(8,128)}), f32[2,64,192]{2,1,0:T(8,128)}) %reduce-scatter.27.cloned.1.call-update) | async-done | bytes 98320 | tf_op jit(solution)/shard_map/reduce_scatter | solution.py:224
  418.3 25.3 %reduce-scatter.25.cloned.1.call-done = f32[2,64,192]{2,1,0:T(8,128)} async-done(((f32[2,256,192]{2,1,0:T(8,128)}), f32[2,64,192]{2,1,0:T(8,128)}) %reduce-scatter.25.cloned.1.call-update) | async-done | bytes 98320 | tf_op jit(solution)/shard_map/reduce_scatter | solution.py:223
  468.5 24.9 %reduce-scatter.37.cloned.1.call-done = f32[96,576]{1,0:T(8,128)} async-done(((f32[384,576]{1,0:T(8,128)}), f32[96,576]{1,0:T(8,128)}) %reduce-scatter.37.cloned.1.call-update) | async-done | bytes 221200
  497.2 26.5 %reduce-scatter.33.cloned.1.call-done = f32[96,768]{1,0:T(8,128)} async-done(((f32[384,768]{1,0:T(8,128)}), f32[96,768]{1,0:T(8,128)}) %reduce-scatter.33.cloned.1.call-update) | async-done | bytes 294928 | tf_op jit(solution)/shard_map/reduce_scatter | solution.py:248
  523.7 30.1 %reduce-scatter.35.cloned.1.call-done = f32[768,96]{0,1:T(8,128)} async-done(((f32[768,384]{0,1:T(8,128)}), f32[768,96]{0,1:T(8,128)}) %reduce-scatter.35.cloned.1.call-update) | async-done | bytes 294928 | tf_op jit(solution)/shard_map/reduce_scatter | solution.py:249
  553.9 54.0 %all-reduce.21.cloned.1.call-done = (f32[3,96,192]{1,2,0:T(8,128)}, f32[192,96]{1,0:T(8,128)}, f32[96,768]{1,0:T(8,128)}, f32[768,96]{0,1:T(8,128)}) async-done(((f32[3,96,192]{1,2,0:T(8,128)}, f32[192,96]{1,0:T(8,128)}, f32[96,768]{1,0:T(8,128)}, f32[768,96]{0,1:T(8,128)}), (f32[3,96,192]{1,2,0:T(8,128)}, f32[192,96]{1,0:T(8,128)}, f32[96,768]{1,0:T(8,128)}, ...) | async-done | bytes 884752 | tf_op jit(solution)/shard_map/psum | solution.py:244
  621.8 43.8 %all_gather.116 = f32[3,384,192]{2,0,1:T(4,128)S(1)} all-gather(f32[3,96,192]{2,0,1:T(4,128)S(1)} %copy.368), channel_id=1, replica_groups=mesh['fsdp'=4,'seq'=4,'tp'=2] {'fsdp'}, dimensions={1}, use_global_device_ids=true | all-gather | bytes 1105920 | tf_op jit(solution)/shard_map/all_gather | solution.py:263
  668.6 10.7 %all-reduce.23.cloned.1.call-done = (f32[128,384]{1,0:T(8,128)}, f32[128,384]{1,0:T(8,128)}, f32[128,384]{1,0:T(8,128)}, f32[128,384]{1,0:T(8,128)}, f32[128,384...) async-done(((f32[128,384]{1,0:T(8,128)}, f32[128,384]{1,0:T(8,128)}, f32[128,384]{1,0:T(8,128)}, f32[128,384]{1,0:T(8,128)}, ...) | async-done | bytes 1572880 | tf_op jit(solution)/shard_map/psum | solution.py:129
  681.0 31.8 %all-gather.12.cloned.1.call-done = f32[768,384]{0,1:T(8,128)} async-done(((f32[768,96]{0,1:T(8,128)}), f32[768,384]{0,1:T(8,128)}) %all-gather.12.cloned.1.call-update) | async-done | bytes 1179664 | tf_op jit(solution)/shard_map/all_gather | solution.py:266
  719.3 14.8 %all_gather.118 = f32[192,384]{0,1:T(8,128)S(1)} all-gather(f32[192,96]{0,1:T(8,128)S(1)} %copy.370), channel_id=1, replica_groups=mesh['fsdp'=4,'seq'=4,'tp'=2] {'fsdp'}, dimensions={1}, use_global_device_ids=true | all-gather | bytes 368640 | tf_op jit(solution)/shard_map/all_gather | solution.py:264
  737.7 13.3 %all-gather.14.cloned.1.call-done = f32[1536,384]{0,1:T(8,128)} async-done(((f32[768,384]{0,1:T(8,128)}), f32[1536,384]{0,1:T(8,128)}) %all-gather.14.cloned.1.call-update) | async-done | bytes 2359312 | tf_op jit(solution)/shard_map/all_gather | solution.py:272
  751.0 46.7 %conditional.1 = (bf16[3,384,384]{2,1,0:T(8,128)(2,1)}, bf16[384,384]{1,0:T(8,128)(2,1)}, bf16[384,1536]{1,0:T(8,128)(2,1)S(1)}, bf16[1536,384]{0,1:T(8,128)(2,1)S(1)}) conditional(s32[]{:T(128)} %clamp.3, f32[3,384,384]{1,2,0:T(8,128)} %all-gather.6.cloned.1.call-done, ...), branch_computations={%region_88.90_spmd, %region_90.92_spmd, %region_92.94_spmd, %regio... | conditional | flops 30601691136 | bytes 88473712 | solution.py:93
  801.1 51.0 %all-reduce.9 = (f32[384]{0:T(512)S(1)}, f32[384]{0:T(512)S(1)}) all-reduce(f32[384]{0:T(512)S(1)} %add_add_fusion.1, f32[384]{0:T(512)S(1)} %add_add_fusion), channel_id=14, replica_groups=mesh['fsdp'=4,'seq'=4,'tp'=2] {'fsdp'}, use_global_device_ids=true, to_apply=%region_81.82.clone | all-reduce | flops 768 | bytes 6144
  852.3 9.8 %all-reduce.7 = (f32[96]{0:T(128)S(1)}, f32[96]{0:T(128)S(1)}) all-reduce(f32[96]{0:T(128)S(1)} %dynamic-slice.24, f32[96]{0:T(128)S(1)} %dynamic-slice.26), channel_id=1, replica_groups=mesh['fsdp'=4,'seq'=4,'tp'=2] {'seq'}, use_global_device_ids=true, to_apply=%region_80.81 | all-reduce | flops 192 | bytes 1536 | tf_op jit(solution)/shard_map/psum | solution.py:244
  868.3 57.8 %all-reduce.29.cloned.1.call-done = (bf16[3,384,384]{2,1,0:T(8,128)(2,1)}, bf16[384,384]{1,0:T(8,128)(2,1)}, bf16[384,1536]{1,0:T(8,128)(2,1)}, bf16[1536,384]{0,1:T(8,128)(2,1)}) async-done(((bf16[3,384,384]{2,1,0:T(8,128)(2,1)}, bf16[384,384]{1,0:T(8,128)(2,1)}, bf16[384,1536]{1,0:T(8,128)(2,1)}, bf16[1536,384]{0,1:T(8,128)(2,1)}), (bf16[3,384,384]{2,1,0:T(8,128)(2,1)}, bf16[384,384]{1,0:T(8,128)(2,1)}, ...) | async-done | bytes 3538960 | tf_op jit(solution)/shard_map/psum | solution.py:279
  (625 shorter events, 236.5 us)
Async XLA Ops:
  7.2 171.1 %all-reduce.27.cloned.1.call-start = ((), (), s32[]{:S(2)}) async-start(), calls=%async_computation.32 | async-start | bytes 1572864 | tf_op jit(solution)/shard_map/psum | solution.py:129
  47.2 76.6 %copy-start.43 = (bf16[128,384]{1,0:T(8,128)(2,1)}, bf16[128,384]{1,0:T(8,128)(2,1)S(1)}, u32[]{:S(2)}) copy-start(bf16[128,384]{1,0:T(8,128)(2,1)S(1)} %get-tuple-element.269) | copy-start | bytes 294916
  146.2 61.1 %all-reduce.25.cloned.1.call-start = ((), (), s32[]{:S(2)}) async-start(), calls=%async_computation.31 | async-start | bytes 1572864 | tf_op jit(solution)/shard_map/psum | solution.py:129
  188.6 105.7 %reduce-scatter.23.cloned.1.call-start = ((), (), s32[]{:S(2)}) async-start(), calls=%async_computation.15 | async-start | bytes 655360 | tf_op jit(solution)/shard_map/reduce_scatter | solution.py:224
  221.4 74.5 %reduce-scatter.21.cloned.1.call-start = ((), (), s32[]{:S(2)}) async-start(), calls=%async_computation.14 | async-start | bytes 655360 | tf_op jit(solution)/shard_map/reduce_scatter | solution.py:223
  229.2 74.3 %reduce-scatter.19.cloned.1.call-start = ((), (), s32[]{:S(2)}) async-start(), calls=%async_computation.13 | async-start | bytes 655360 | tf_op jit(solution)/shard_map/reduce_scatter | solution.py:224
  234.3 97.0 %reduce-scatter.17.cloned.1.call-start = ((), (), s32[]{:S(2)}) async-start(), calls=%async_computation.12 | async-start | bytes 655360 | tf_op jit(solution)/shard_map/reduce_scatter | solution.py:223
  242.3 117.6 %reduce-scatter.31.cloned.1.call-start = ((), (), s32[]{:S(2)}) async-start(), calls=%async_computation.19 | async-start | bytes 655360 | tf_op jit(solution)/shard_map/reduce_scatter | solution.py:224
  245.8 142.0 %reduce-scatter.29.cloned.1.call-start = ((), (), s32[]{:S(2)}) async-start(), calls=%async_computation.18 | async-start | bytes 655360 | tf_op jit(solution)/shard_map/reduce_scatter | solution.py:223
  253.6 162.2 %reduce-scatter.27.cloned.1.call-start = ((), (), s32[]{:S(2)}) async-start(), calls=%async_computation.17 | async-start | bytes 655360 | tf_op jit(solution)/shard_map/reduce_scatter | solution.py:224
  265.0 178.6 %reduce-scatter.25.cloned.1.call-start = ((), (), s32[]{:S(2)}) async-start(), calls=%async_computation.16 | async-start | bytes 655360 | tf_op jit(solution)/shard_map/reduce_scatter | solution.py:223
  280.4 186.5 %reduce-scatter.39.cloned.1.call-start = ((), (), s32[]{:S(2)}) async-start(), calls=%async_computation.28 | async-start | bytes 491520
  294.2 199.2 %reduce-scatter.37.cloned.1.call-start = ((), (), s32[]{:S(2)}) async-start(), calls=%async_computation.27 | async-start | bytes 1228800
  304.5 141.6 %copy-start.40 = (bf16[128,384]{1,0:T(8,128)(2,1)S(1)}, bf16[128,384]{1,0:T(8,128)(2,1)}, u32[]{:S(2)}) copy-start(bf16[128,384]{1,0:T(8,128)(2,1)} %copy-done.39) | copy-start | bytes 294916
  360.9 87.4 %copy-start.77 = (bf16[1,128,192]{1,2,0:T(8,128)(2,1)}, bf16[1,128,192]{1,2,0:T(8,128)(2,1)S(1)}, u32[]{:S(2)}) copy-start(bf16[1,128,192]{1,2,0:T(8,128)(2,1)S(1)} %copy.365) | copy-start | bytes 147460
  453.0 70.7 %reduce-scatter.33.cloned.1.call-start = ((), (), s32[]{:S(2)}) async-start(), calls=%async_computation.25 | async-start | bytes 1474560 | tf_op jit(solution)/shard_map/reduce_scatter | solution.py:248
  456.0 97.8 %reduce-scatter.35.cloned.1.call-start = ((), (), s32[]{:S(2)}) async-start(), calls=%async_computation.26 | async-start | bytes 1474560 | tf_op jit(solution)/shard_map/reduce_scatter | solution.py:249
  459.6 148.3 %all-reduce.21.cloned.1.call-start = ((), (), s32[]{:S(2)}) async-start(), calls=%async_computation.29 | async-start | bytes 1966080 | tf_op jit(solution)/shard_map/psum | solution.py:244
  553.8 113.5 %all-gather.8.cloned.1.call-start = ((), (), s32[]{:S(2)}) async-start(), calls=%async_computation.21 | async-start | bytes 1474560 | tf_op jit(solution)/shard_map/all_gather | solution.py:265
  609.8 69.5 %all-reduce.23.cloned.1.call-start = ((), (), s32[]{:S(2)}) async-start(), calls=%async_computation.30 | async-start | bytes 3145728 | tf_op jit(solution)/shard_map/psum | solution.py:129
  619.7 93.2 %all-gather.12.cloned.1.call-start = ((), (), s32[]{:S(2)}) async-start(), calls=%async_computation.23 | async-start | bytes 1474560 | tf_op jit(solution)/shard_map/all_gather | solution.py:266
  620.6 116.5 %all-gather.6.cloned.1.call-start = ((), (), s32[]{:S(2)}) async-start(), calls=%async_computation.20 | async-start | bytes 2654208 | tf_op jit(solution)/shard_map/all_gather | solution.py:269
  667.2 70.5 %all-gather.10.cloned.1.call-start = ((), (), s32[]{:S(2)}) async-start(), calls=%async_computation.22 | async-start | bytes 3538944 | tf_op jit(solution)/shard_map/all_gather | solution.py:271
  667.8 83.2 %all-gather.14.cloned.1.call-start = ((), (), s32[]{:S(2)}) async-start(), calls=%async_computation.24 | async-start | bytes 3538944 | tf_op jit(solution)/shard_map/all_gather | solution.py:272
  712.9 213.2 %all-reduce.29.cloned.1.call-start = ((), (), s32[]{:S(2)}) async-start(), calls=%async_computation.33 | async-start | bytes 7077888 | tf_op jit(solution)/shard_map/psum | solution.py:279
  799.1 66.3 %copy-start.143 = (f32[96]{0:T(128)S(1)}, f32[96]{0:T(128)}, u32[]{:S(2)}) copy-start(f32[96]{0:T(128)} %param.35) | copy-start | bytes 1156
  799.2 66.8 %copy-start.145 = (f32[96]{0:T(128)S(1)}, f32[96]{0:T(128)}, u32[]{:S(2)}) copy-start(f32[96]{0:T(128)} %param.36) | copy-start | bytes 1156
  799.2 66.8 %copy-start.146 = (f32[96]{0:T(128)S(1)}, f32[96]{0:T(128)}, u32[]{:S(2)}) copy-start(f32[96]{0:T(128)} %param.42) | copy-start | bytes 1156
  799.2 68.2 %copy-start.38 = (f32[3,96,192]{1,2,0:T(8,128)S(1)}, f32[3,96,192]{1,2,0:T(8,128)}, u32[]{:S(2)}) copy-start(f32[3,96,192]{1,2,0:T(8,128)} %get-tuple-element.284) | copy-start | bytes 663556
  799.2 126.9 %copy-start.33 = (f32[3,96,192]{2,1,0:T(8,128)S(1)}, f32[3,96,192]{2,1,0:T(8,128)}, u32[]{:S(2)}) copy-start(f32[3,96,192]{2,1,0:T(8,128)} %param.31) | copy-start | bytes 663556
  862.2 67.3 %copy-start.35 = (f32[96,768]{1,0:T(8,128)S(1)}, f32[96,768]{1,0:T(8,128)}, u32[]{:S(2)}) copy-start(f32[96,768]{1,0:T(8,128)} %param.33) | copy-start | bytes 884740
  863.5 67.7 %copy-start.37 = (f32[768,96]{0,1:T(8,128)S(1)}, f32[768,96]{0,1:T(8,128)}, u32[]{:S(2)}) copy-start(f32[768,96]{0,1:T(8,128)} %param.34) | copy-start | bytes 884740
  (134 other events, 1913.9 us)
Sparse Core Ops, SparseCore 0:
  146.4 17.8 all-reduce.26
  188.7 18.5 all-reduce.24
  221.5 26.3 reduce-scatter.22
  250.6 25.0 reduce-scatter.20
  278.4 25.1 reduce-scatter.18
  306.2 25.1 reduce-scatter.16
  334.7 25.0 reduce-scatter.30
  362.7 25.1 reduce-scatter.28
  390.7 25.1 reduce-scatter.26
  418.5 25.0 reduce-scatter.24
  445.9 20.9 reduce-scatter.38
  469.1 24.3 reduce-scatter.36
  495.8 27.8 reduce-scatter.32
  525.8 27.9 reduce-scatter.34
  557.6 50.2 all-reduce.20
  610.0 44.3 all-gather.7
  658.2 21.0 all-reduce.22
  681.3 31.4 all-gather.11
  714.4 9.3 all-gather.5
  725.2 12.5 all-gather.9
  739.3 11.7 all-gather.13
  799.3 126.7 all-reduce.28
where the time goes:
time: 950 us; the launch traced here: 940 us
  waiting for transfers between devices  413 us (43%)
  blocking collectives  267 us (28%)
  matrix products  104 us (11%)
  local copies, waits for them, and re-layouts  63.6 us (7%)
  other arithmetic  49.8 us (5%)
  loops' own time  23.4 us (2%)
  between operations  18.6 us (2%)
    reduce_scatter x4, waiting for transfers between devices, body(): lax.psum_scatter(key_part, 'seq', scatter_dimension=1, tiled=True)  79 us
    unnamed x2, blocking collectives  65 us
    psum x1, waiting for transfers between devices, body(): lax.psum(shortened(mine), ('fsdp', 'tp'))  57.8 us
    reduce_scatter x4, waiting for transfers between devices, body(): lax.psum_scatter(value_part, 'seq', scatter_dimension=1, tiled=True)  57 us
    psum x1, waiting for transfers between devices, body(): lax.psum((sum_qkv, sum_out, sum_up, sum_down, sum_attn, sum_ffn), 'seq')  54 us
    all_gather x1, blocking collectives, body(): lax.all_gather(new_moment_qkv, 'fsdp', axis=1, tiled=True)  43.8 us
    all_gather x4, blocking collectives, body(): keys_all = lax.all_gather(keys_loc, 'seq', axis=1, tiled=True)  37.8 us
    unnamed x24, waiting for transfers between devices  33 us
  transfers between devices with their start and end apart: 22, of which 17 were waited for; matrix products, arithmetic and copies ran while one was open for 14% of the time, Pallas kernels for 0%

commit v1 on v0

v1 whole, which is shorter than its diff:
```python
import functools

import jax
import jax.numpy as jnp
from jax import lax
from jax.experimental import pallas as pl
from jax.experimental.pallas import tpu as pltpu
from jax.sharding import PartitionSpec as P

F32 = jnp.float32
BF16 = jnp.bfloat16
MESH = pl.DeviceIdType.MESH
def place():
    rep = lax.axis_size("fsdp") // 4
    fi, s, t = lax.axis_index("fsdp"), lax.axis_index("seq"), lax.axis_index("tp")
    z, fr = fi // rep, lax.rem(fi, rep)
    return rep, z, fr, s, t


def remote(src, dst, ss, rs, dev):
    return pltpu.make_async_remote_copy(src_ref=src, dst_ref=dst, send_sem=ss, recv_sem=rs, device_id=dev, device_id_type=MESH)


def gather_kernel(tok, go, wsh, gsh, w, gains, xo, go_o,
                  zs, zr, pls, plr, pps, ppr, gss, gsr, ts, tr, loc):
    rep, z, fr, s, t = place()
    y, x = s // 2, lax.rem(s, 2)
    zdev = lambda k: {"fsdp": lax.rem(z + k, 4) * rep + fr}
    def sdev(j):
        yy, xx = y, x
        if j & 2: yy = 1 - y
        if j & 1: xx = 1 - x
        return yy * 2 + xx
    other = {"tp": 1 - t}

    bar = pltpu.get_barrier_semaphore()
    for k in range(1, 4):
        pl.semaphore_signal(bar, inc=1, device_id=zdev(k), device_id_type=MESH)
    for j in range(1, 4):
        pl.semaphore_signal(bar, inc=1, device_id={"seq": sdev(j)}, device_id_type=MESH)
    pl.semaphore_signal(bar, inc=1, device_id=other, device_id_type=MESH)
    pl.semaphore_wait(bar, 7)

    def rows(zz, yy=None):
        if yy is None:
            return pl.ds(pl.multiple_of(zz * 96, 32), 96)
        return pl.ds(pl.multiple_of(zz * 96 + yy * 48, 16), 48)
    def cols(tt, xx=None):
        if xx is None:
            return pl.ds(pl.multiple_of(tt * 768, 128), 768)
        return pl.ds(pl.multiple_of(tt * 768 + xx * 384, 128), 384)

    sends = []
    def go_(c):
        c.start(); sends.append(c); return c

    zc = {}
    for m in range(3):
        for k in range(1, 4):
            src = wsh.at[m, pl.ds(pl.multiple_of(y * 48, 16), 48), pl.ds(pl.multiple_of(x * 384, 128), 384)]
            zc[m, k] = go_(remote(src, w.at[m, rows(z, y), cols(t, x)], zs.at[m, k - 1], zr.at[m, k - 1], zdev(k)))
        if m == 0:
            gc = [go_(remote(gsh, gains.at[k], gss.at[k - 1], gsr.at[k - 1], zdev(k))) for k in range(1, 4)]
            tc = []
            for j in range(1, 4):
                for a, (src, dst) in enumerate(((tok, xo), (go, go_o))):
                    tc.append(go_(remote(src.at[sdev(j), t], dst.at[pl.ds(pl.multiple_of(s * 64, 64), 64)], ts.at[a, j - 1], tr.at[a, j - 1], {"seq": sdev(j)})))
    own = []
    for m in range(3):
        own.append(go_(remote(wsh.at[m], w.at[m, rows(z), cols(t)], pps.at[m, 0], ppr.at[m, 0], other)))
    lc = []
    for a, (src, dst) in enumerate(((tok, xo), (go, go_o))):
        lc.append(pltpu.make_async_copy(src.at[s, t], dst.at[pl.ds(pl.multiple_of(s * 64, 64), 64)], loc.at[a]))
    for m in range(3):
        lc.append(pltpu.make_async_copy(wsh.at[m], w.at[m, rows(z), cols(t)], loc.at[2 + m]))
    lc.append(pltpu.make_async_copy(gsh, gains.at[0], loc.at[5]))
    for c in lc:
        c.start()

    pc = {}
    for m in range(3):
        for k in range(1, 4):
            zc[m, k].wait_recv()
            zk = lax.rem(z + 4 - k, 4)
            blk = w.at[m, rows(zk, y), cols(t, x)]
            for j in range(1, 4):
                pc[m, k, j] = go_(remote(blk, blk, pls.at[m, k - 1, j - 1], plr.at[m, k - 1, j - 1], {"seq": sdev(j)}))
    pp = {}
    for m in range(3):
        for k in range(1, 4):
            for j in range(1, 4):
                pc[m, k, j].wait_recv()
            zk = lax.rem(z + 4 - k, 4)
            blk = w.at[m, rows(zk), cols(t)]
            pp[m, k] = go_(remote(blk, blk, pps.at[m, k], ppr.at[m, k], other))
    for m in range(3):
        own[m].wait_recv()
        for k in range(1, 4):
            pp[m, k].wait_recv()
    for c in gc + tc:
        c.wait_recv()
    for c in lc:
        c.wait()
    for c in sends:
        c.wait_send()


def gather(tok, go, wsh, gsh):
    vm = pl.BlockSpec(memory_space=pltpu.VMEM)
    d = wsh.shape[-1] // 2
    D = pltpu.SemaphoreType.DMA
    return pl.pallas_call(
        gather_kernel,
        out_shape=(jax.ShapeDtypeStruct((3, d, 4 * d), BF16), jax.ShapeDtypeStruct((4,) + gsh.shape, BF16),
                   jax.ShapeDtypeStruct((4 * tok.shape[2], d), BF16), jax.ShapeDtypeStruct((4 * tok.shape[2], d), BF16)),
        in_specs=[vm] * 4, out_specs=(vm,) * 4,
        scratch_shapes=[D((3, 3)), D((3, 3)), D((3, 3, 3)), D((3, 3, 3)), D((3, 4)), D((3, 4)), D((3,)), D((3,)), D((2, 3)), D((2, 3)), D((6,))],
        compiler_params=pltpu.CompilerParams(collective_id=0, has_side_effects=True, vmem_limit_bytes=60000 * 1024),
        name="gather",
    )(tok, go, wsh, gsh)


def mm(a, b):
    return jnp.dot(a, b, preferred_element_type=F32)


def mm_nt(a, b):
    return lax.dot_general(a, b, (((1,), (1,)), ((), ())), preferred_element_type=F32)


def mm_tn(a, b):
    return lax.dot_general(a, b, (((0,), (0,)), ((), ())), preferred_element_type=F32)


def stats(v):
    center = v - jnp.mean(v, axis=-1, keepdims=True)
    inv = lax.rsqrt(jnp.mean(center * center, axis=-1, keepdims=True) + 1e-06)
    return center * inv, inv


def norm_back(up, plain, inv, gain):
    e = up * gain
    return inv * (
        e - jnp.mean(e, axis=-1, keepdims=True) - plain * jnp.mean(e * plain, axis=-1, keepdims=True)
    )


def compute_kernel(
    len_ref, x_ref, g_ref, w_ref, gains_ref,
    out_ref, ig_ref, raw_ref, gsum_ref,
    wn, qkv, wts, prb, att, back, natr, raw_n,
):
    length = len_ref[0]
    lanes = lax.broadcasted_iota(jnp.int32, (1, 128), 1)
    low = lanes < 64
    half = 768

    for i, (tile, mixed, first) in enumerate(((0, 2, True), (1, 2, False), (3, 5, True), (4, 5, False))):
        wn[i, :, 0:128] = w_ref[0, :, tile * 128 : tile * 128 + 128]
        wn[i, :, 256:384] = w_ref[0, :, half + tile * 128 : half + tile * 128 + 128]
        a = w_ref[0, :, mixed * 128 : mixed * 128 + 128]
        b = w_ref[0, :, half + mixed * 128 : half + mixed * 128 + 128]
        if first:
            wn[i, :, 128:256] = jnp.where(low, a, b)
        else:
            m = jnp.where(low, b, a).astype(F32)
            wn[i, :, 128:256] = pltpu.roll(m, 64, 1).astype(BF16)

    gains = gains_ref[0].astype(F32)
    for k in range(1, gains_ref.shape[0]):
        gains = gains + gains_ref[k].astype(F32)
    attn_use, ffn_use = gains[0:1], gains[1:2]

    x = x_ref[...].astype(F32)
    plain_attn, inv_attn = stats(x)
    norm_attn = (plain_attn * attn_use).astype(BF16)
    for i in range(3):
        qkv[i] = mm(norm_attn, wn[i]).astype(BF16)
    natr[0] = norm_attn.astype(F32).T.astype(BF16)

    rows = x.shape[0]
    valid = lax.broadcasted_iota(jnp.int32, (rows, 1), 0) < length
    scale = 64 ** (-0.5)

    for p in range(3):
        sl = slice(p * 128, p * 128 + 128)
        q, k, v = qkv[0, :, sl], qkv[1, :, sl], qkv[2, :, sl]
        parts = []
        for h in range(2):
            sel = low if h == 0 else ~low
            s = mm_nt(k, jnp.where(sel, q, jnp.zeros_like(q))) * scale
            s = jnp.where(valid, s, -jnp.inf)
            top = jnp.max(s, axis=0, keepdims=True)
            e = jnp.exp(s - top)
            w = e * (1.0 / jnp.sum(e, axis=0, keepdims=True))
            wts[2 * p + h] = w
            pb = w.astype(BF16)
            prb[2 * p + h] = pb
            parts.append(mm_tn(pb, v))
        att[:, sl] = jnp.where(low, parts[0], parts[1]).astype(BF16)

    middle = x + mm_nt(att[...], wn[3])
    plain_ffn, inv_ffn = stats(middle)
    norm_ffn = (plain_ffn * ffn_use).astype(BF16)
    natr[1] = norm_ffn.astype(F32).T.astype(BF16)
    upstream = g_ref[...]
    natr[2] = upstream.astype(F32).T.astype(BF16)

    acc_out = jnp.zeros((rows, x.shape[1]), F32)
    acc_back = jnp.zeros((rows, x.shape[1]), F32)
    width = 256
    for c in range(1536 // width):
        cs = slice(c * width, c * width + width)
        hidden = mm(norm_ffn, w_ref[1, :, cs])
        cdf = 0.5 * (1.0 + lax.erf(hidden * 0.7071067811865476))
        act = (hidden * cdf).astype(BF16)
        back_act = mm(upstream, w_ref[2, :, cs])
        pdf = 0.3989422804014327 * jnp.exp(-0.5 * hidden * hidden)
        bh = (back_act * (cdf + hidden * pdf)).astype(BF16)
        acc_out = acc_out + mm_nt(act, w_ref[2, :, cs])
        acc_back = acc_back + mm_nt(bh, w_ref[1, :, cs])
        raw_ref[1, :, cs] = mm(natr[1], bh).astype(BF16)
        raw_ref[2, :, cs] = mm(natr[2], act).astype(BF16)
    out_ref[...] = (middle + acc_out).astype(BF16)

    gsum_ref[...] = jnp.zeros_like(gsum_ref)
    gsum_ref[1:2, :] = jnp.sum(acc_back * plain_ffn, axis=0, keepdims=True)
    back_middle = upstream.astype(F32) + norm_back(acc_back, plain_ffn, inv_ffn, ffn_use)
    mh = back_middle.astype(BF16)
    raw_n[3] = mm(back_middle.astype(BF16).astype(F32).T.astype(BF16), att[...]).astype(F32)
    ba = mm(mh, wn[3]).astype(BF16)

    for p in range(3):
        sl = slice(p * 128, p * 128 + 128)
        q, k, v = qkv[0, :, sl], qkv[1, :, sl], qkv[2, :, sl]
        bap = ba[:, sl]
        bq, bk, bv = [], [], []
        for h in range(2):
            sel = low if h == 0 else ~low
            bp = mm_nt(v, jnp.where(sel, bap, jnp.zeros_like(bap)))
            w = wts[2 * p + h]
            delta = jnp.sum(w * bp, axis=0, keepdims=True)
            ds = (w * (bp - delta) * scale).astype(BF16)
            bq.append(mm_tn(ds, k))
            bk.append(mm(ds, q))
            bv.append(mm(prb[2 * p + h], bap))
        back[0, :, sl] = jnp.where(low, bq[0], bq[1]).astype(BF16)
        back[1, :, sl] = jnp.where(low, bk[0], bk[1]).astype(BF16)
        back[2, :, sl] = jnp.where(low, bv[0], bv[1]).astype(BF16)

    back_attn = jnp.zeros((rows, x.shape[1]), F32)
    for i in range(3):
        b = back[i]
        raw_n[i] = mm(natr[0], b)
        back_attn = back_attn + mm_nt(b, wn[i])
    gsum_ref[0:1, :] = jnp.sum(back_attn * plain_attn, axis=0, keepdims=True)
    ig_ref[...] = (back_middle + norm_back(back_attn, plain_attn, inv_attn, attn_use)).astype(BF16)

    for a, b, tile, mixed in ((0, 1, 0, 2), (2, 3, 3, 5)):
        for i, tl in ((a, tile), (b, tile + 1)):
            raw_ref[0, :, tl * 128 : tl * 128 + 128] = raw_n[i, :, 0:128].astype(BF16)
            raw_ref[0, :, half + tl * 128 : half + tl * 128 + 128] = raw_n[i, :, 256:384].astype(BF16)
        first = raw_n[a, :, 128:256]
        second = pltpu.roll(raw_n[b, :, 128:256], 64, 1)
        raw_ref[0, :, mixed * 128 : mixed * 128 + 128] = jnp.where(low, first, second).astype(BF16)
        raw_ref[0, :, half + mixed * 128 : half + mixed * 128 + 128] = jnp.where(low, second, first).astype(BF16)


def compute(length, x, g, w, gains):
    d = x.shape[1]
    rows = x.shape[0]
    vm = pl.BlockSpec(memory_space=pltpu.VMEM)
    return pl.pallas_call(
        compute_kernel,
        out_shape=(
            jax.ShapeDtypeStruct((rows, d), BF16),
            jax.ShapeDtypeStruct((rows, d), BF16),
            jax.ShapeDtypeStruct((3, d, 4 * d), BF16),
            jax.ShapeDtypeStruct((8, d), F32),
        ),
        in_specs=[pl.BlockSpec(memory_space=pltpu.SMEM), vm, vm, vm, vm],
        out_specs=(vm, vm, vm, vm),
        scratch_shapes=[
            pltpu.VMEM((4, d, d), BF16),
            pltpu.VMEM((3, rows, d), BF16),
            pltpu.VMEM((6, rows, rows), F32),
            pltpu.VMEM((6, rows, rows), BF16),
            pltpu.VMEM((rows, d), BF16),
            pltpu.VMEM((3, rows, d), BF16),
            pltpu.VMEM((3, d, rows), BF16),
            pltpu.VMEM((4, d, d), F32),
        ],
        compiler_params=pltpu.CompilerParams(vmem_limit_bytes=60000 * 1024),
        name="image",
    )(length, x, g, w, gains)


def pack_cols(q, k, v, o, t):
    def sp(a):
        if t == 0:
            return a[:, 0:128], a[:, 128:192]
        return a[:, 64:192], a[:, 0:64]
    (qp, q2), (kp, k2), (vp, v2), (op, o2) = sp(q), sp(k), sp(v), sp(o)
    if t == 0:
        return jnp.concatenate([qp, kp, q2, k2, vp, op, v2, o2], axis=1)
    return jnp.concatenate([qp, kp, k2, q2, vp, op, o2, v2], axis=1)


def unpack_cols(a, t):
    c = lambda lo, n: a[:, lo : lo + n]
    if t == 0:
        q = jnp.concatenate([c(0, 128), c(256, 64)], 1)
        k = jnp.concatenate([c(128, 128), c(320, 64)], 1)
        v = jnp.concatenate([c(384, 128), c(640, 64)], 1)
        o = jnp.concatenate([c(512, 128), c(704, 64)], 1)
    else:
        q = jnp.concatenate([c(320, 64), c(0, 128)], 1)
        k = jnp.concatenate([c(256, 64), c(128, 128)], 1)
        v = jnp.concatenate([c(704, 64), c(384, 128)], 1)
        o = jnp.concatenate([c(640, 64), c(512, 128)], 1)
    return q, k, v, o


def split(a):
    hi = a.astype(BF16)
    return hi, (a - hi.astype(F32)).astype(BF16)


def dot3(a, b):
    (ah, al), (bh, bl) = a, b
    return mm(ah, bh) + (mm(ah, bl) + mm(al, bh))


def dot3c(a, b):
    (ah, al), (bh, bl) = a, b
    return mm(jnp.concatenate([ah, ah, al], 1), jnp.concatenate([bh, bl, bh], 0))


def ns(m_ref, d_ref, q_hi, q_lo, d3):
    m = m_ref[...]
    gram = mm_nt(m, m)
    n = gram.shape[0]
    eye = lax.broadcasted_iota(jnp.int32, (n, n), 0) == lax.broadcasted_iota(jnp.int32, (n, n), 1)
    total = jnp.sum(jnp.where(eye, gram, 0.0))
    inv = 1.0 / (jnp.sqrt(total) + 1e-07)
    gram = gram * (inv * inv)
    ident = jnp.where(eye, 3.4445, 0.0)

    def poly(gs, gram):
        return ident + (-4.775 * gram + 2.0315 * d3(gs, gs))
    q = None
    for it in range(5):
        gs = split(gram)
        r = poly(gs, gram)
        rs = split(r)
        q = r if q is None else d3(rs, split(q))
        if it < 4:
            gram = d3(split(d3(rs, rs)), gs)
    qh, ql = split(q)
    q_hi[...] = qh
    q_lo[...] = ql
    for c in range(0, m_ref.shape[1], 256):
        cs = slice(c, c + 256)
        d_ref[:, cs] = ((mm(q_hi[...], m_ref[:, cs]) + mm(q_lo[...], m_ref[:, cs])) * inv).astype(BF16)


def run(m, which):
    d3 = {'3': dot3, 'c': dot3c}[which]
    vm = pl.BlockSpec(memory_space=pltpu.VMEM)
    return pl.pallas_call(lambda *r: ns(*r, d3), out_shape=jax.ShapeDtypeStruct(m.shape, BF16), in_specs=[vm], out_specs=vm,
      scratch_shapes=[pltpu.VMEM((m.shape[0],)*2, BF16)]*2, compiler_params=pltpu.CompilerParams(vmem_limit_bytes=60000*1024), name="ns")(m)


OWNERS = ((1, 0, 0), (2, 3, 0), (1, 1, 0), (2, 1, 0), (1, 2, 0), (2, 2, 0))
def newton_schulz(role, mbuf, dbuf, q_hi, q_lo):
    wide = (role == 0) | (role == 1)
    first = (role == 2) | (role == 4)
    col = lax.broadcasted_iota(jnp.int32, (1, mbuf.shape[1]), 1)
    right = col >= 384
    cc = jnp.where(right, col - 384, col)
    lead = (cc < 128) | ((cc >= 256) & (jnp.where(right, 1, 0) == jnp.where(cc >= 320, 1, 0)))
    pick = jnp.where(lead, 1, 0)
    keep = jnp.where(wide, 1, jnp.where(col >= 768, 0, jnp.where(first, pick, 1 - pick)))
    zero = jnp.zeros((), BF16)
    n = mbuf.shape[0]
    gram = jnp.zeros((n, n), F32)
    for c in range(0, mbuf.shape[1], 512):
        m = jnp.where(keep[:, c : c + 512] > 0, mbuf[:, c : c + 512], zero)
        mbuf[:, c : c + 512] = m
        gram = gram + mm_nt(m, m)
    eye = lax.broadcasted_iota(jnp.int32, (n, n), 0) == lax.broadcasted_iota(jnp.int32, (n, n), 1)
    inv = 1.0 / (jnp.sqrt(jnp.sum(jnp.where(eye, gram, 0.0))) + 1e-07)
    gram = gram * (inv * inv)
    ident = jnp.where(eye, 3.4445, 0.0)
    q = None
    for it in range(5):
        gs = split(gram)
        r = ident + (-4.775 * gram + 2.0315 * dot3c(gs, gs))
        rs = split(r)
        q = r if q is None else dot3c(rs, split(q))
        if it < 4:
            gram = dot3c(split(dot3c(rs, rs)), gs)
    qh, ql = split(q)
    q_hi[...] = qh
    q_lo[...] = ql
    fac = inv * jnp.where(role == 1, 1.0, 0.5)
    for c in range(0, mbuf.shape[1], 256):
        m = mbuf[:, c : c + 256]
        dbuf[:, c : c + 256] = ((mm(q_hi[...], m) + mm(q_lo[...], m)) * fac).astype(BF16)


def reduce_kernel(scale, raw, gs, mom, bo, ig,
                  grad_sh, delta_sh, bo_out, ig_out, gs_out,
                  pr, acc, sx, xr, sy, yr, sz, zr, mb, mbuf, dbuf, dpc, q_hi, q_lo, g1, g2, g3, gz, gst,
                  ps_s, ps_r, x_s, x_r, y_s, y_r, z_s, z_r, a_s, a_r, o_s, m_r, d_s, d_r, e_s, e_r, t_s, t_r, g_s, g_r, loc):
    rep, z, fr, s, t = place()
    y, x = s // 2, lax.rem(s, 2)
    def zdev(k):
        return {"fsdp": lax.rem(z + k, 4) * rep + fr}
    def sidx(j):
        yy, xx = y, x
        if j & 2: yy = 1 - y
        if j & 1: xx = 1 - x
        return yy * 2 + xx
    def sdev(j):
        return {"seq": sidx(j)}
    other = {"tp": 1 - t}
    me = z * 8 + s * 2 + t
    def dev(i):
        return {"fsdp": (i // 8) * rep + fr, "seq": lax.rem(i // 2, 4), "tp": lax.rem(i, 2)}

    bar = pltpu.get_barrier_semaphore()
    def greet(i, carry):
        pl.semaphore_signal(bar, inc=1, device_id=dev(lax.rem(me + i, 32)), device_id_type=MESH)
        return carry
    lax.fori_loop(1, 32, greet, 0)
    pl.semaphore_wait(bar, 31)

    r48 = lambda yy: pl.ds(pl.multiple_of(yy * 48, 16), 48)
    r96 = lambda zz, yy: pl.ds(pl.multiple_of(zz * 96 + yy * 48, 16), 48)
    c384 = lambda xx: pl.ds(pl.multiple_of(xx * 384, 128), 384)
    c768 = lambda tt: pl.ds(pl.multiple_of(tt * 768, 128), 768)

    sends = []
    def go(c):
        c.start()
        sends.append(c)
        return c

    order = (1, 2, 0)
    pc = {m: go(remote(raw.at[m, :, c768(1 - t)], pr.at[m], ps_s.at[m], ps_r.at[m], other)) for m in order}
    gc = go(remote(gs, g1, g_s.at[0], g_r.at[0], other))
    xc = {}
    for m in order:
        pc[m].wait_recv()
        theirs = pl.ds(pl.multiple_of(t * 768 + (1 - x) * 384, 128), 384)
        sx[m] = (raw[m, :, theirs].astype(F32) + pr[m, :, c384(1 - x)].astype(F32)).astype(BF16)
        xc[m] = go(remote(sx.at[m], xr.at[m], x_s.at[m], x_r.at[m], sdev(1)))
        mine = pl.ds(pl.multiple_of(t * 768 + x * 384, 128), 384)
        acc[m] = raw[m, :, mine].astype(F32) + pr[m, :, c384(x)].astype(F32)
    gc.wait_recv()
    gst[0] = gs[...] + g1[...]
    gc = go(remote(gst.at[0], g2, g_s.at[1], g_r.at[1], sdev(1)))
    yc = {}
    for m in order:
        xc[m].wait_recv()
        for f in range(4):
            rr = pl.ds(pl.multiple_of(f * 96 + (1 - y) * 48, 16), 48)
            sy[m, f] = (acc[m, rr, :] + xr[m, rr, :].astype(F32)).astype(BF16)
        yc[m] = go(remote(sy.at[m], yr.at[m], y_s.at[m], y_r.at[m], sdev(2)))
        for f in range(4):
            rr = pl.ds(pl.multiple_of(f * 96 + y * 48, 16), 48)
            acc[m, rr, :] = acc[m, rr, :] + xr[m, rr, :].astype(F32)
    gc.wait_recv()
    gst[1] = gst[0] + g2[...]
    gc = go(remote(gst.at[1], g3, g_s.at[2], g_r.at[2], sdev(2)))
    zc = {}
    for m in order:
        yc[m].wait_recv()
        for k in range(1, 4):
            zk = lax.rem(z + k, 4)
            sz[m, k - 1] = (acc[m, r96(zk, y), :] + yr[m, zk].astype(F32)).astype(BF16)
            zc[m, k] = go(remote(sz.at[m, k - 1], zr.at[m, k - 1], z_s.at[m, k - 1], z_r.at[m, k - 1], zdev(k)))
    gc.wait_recv()
    gz[pl.ds(z, 1)] = (gst[1] + g3[...])[None]
    gcs = []
    for k in range(1, 4):
        gcs.append(go(remote(gz.at[z], gz.at[z], g_s.at[2 + k], g_r.at[2 + k], zdev(k))))

    def owner_dev(o):
        zo, so, to = OWNERS[o]
        return {"fsdp": zo * rep + fr, "seq": so, "tp": to}
    def am(o):
        zo, so, to = OWNERS[o]
        return (z == zo) & (s == so) & (t == to)

    def piece(src, o, dst, i, cond=None):
        mine = am(o)
        far = ~mine if cond is None else (~mine) & cond
        near = mine if cond is None else mine & cond
        @pl.when(far)
        def _():
            remote(src, dst, o_s.at[i], m_r.at[me], owner_dev(o)).start()
        @pl.when(near)
        def _():
            pltpu.make_async_copy(src, dst, m_r.at[me]).start()
        def fin():
            @pl.when(far)
            def _():
                remote(src, dst, o_s.at[i], m_r.at[me], owner_dev(o)).wait_send()
        return fin

    fins = []
    ac = []
    for m in order:
        tot = acc[m, r96(z, y), :] + yr[m, z].astype(F32)
        for k in range(1, 4):
            zc[m, k].wait_recv()
            tot = tot + zr[m, k - 1].astype(F32)
        grad_sh[m, r48(y), c384(x)] = (tot * scale).astype(BF16)
        blk = grad_sh.at[m, r48(y), c384(x)]
        gb = grad_sh[m, r48(y), c384(x)].astype(F32)
        mb[m] = (0.5 * mom[m, r48(y), c384(x)] + gb).astype(BF16)
        wide = mbuf.at[r96(z, y), pl.ds(pl.multiple_of(t * 768 + x * 384, 128), 384)]
        narrow = mbuf.at[r96(z, y), c384(t)]
        if m == 1:
            fins.append(piece(mb.at[m], 0, wide, 0))
        elif m == 2:
            fins.append(piece(mb.at[m], 1, wide, 1))
        else:
            fins.append(piece(mb.at[m], 2, narrow, 2, x == 0))
            fins.append(piece(mb.at[m], 3, narrow, 3, x == 0))
            fins.append(piece(mb.at[m], 4, narrow, 2, x == 1))
            fins.append(piece(mb.at[m], 5, narrow, 3, x == 1))
        for j in range(1, 4):
            ac.append(go(remote(blk, blk, a_s.at[m, j - 1], a_r.at[m, j - 1], sdev(j))))
    for k in range(1, 4):
        gcs[k - 1].wait_recv()
    gs_out[...] = ((gz[0] + gz[1]) + (gz[2] + gz[3])) * scale

    lc = []
    for a, (src, dst) in enumerate(((bo, bo_out), (ig, ig_out))):
        for j in range(4):
            sj = sidx(j)
            blk = src.at[pl.ds(pl.multiple_of(sj * 64, 64), 64)]
            if j:
                go(remote(blk, dst.at[s, t], t_s.at[a, j, 0], t_r.at[a, j, 0], {"seq": sj}))
            else:
                lc.append(pltpu.make_async_copy(blk, dst.at[s, t], loc.at[a]))
                lc[-1].start()
            go(remote(blk, dst.at[s, t], t_s.at[a, j, 1], t_r.at[a, j, 1], {"seq": sj, "tp": 1 - t}))

    role = jnp.int32(-1)
    for o in range(6):
        role = jnp.where(am(o), o, role)
    slot = jnp.where(role == 0, 1, jnp.where(role == 1, 2, jnp.where((role == 2) | (role == 4), 0, 3)))
    xo = jnp.where(role >= 4, 1, 0)

    def involved(i):
        return (role < 2) | (lax.rem(i // 2, 2) == xo)

    def own_region(ref, i):
        zz, ss, tt = i // 8, lax.rem(i // 2, 4), lax.rem(i, 2)
        yy, xx = ss // 2, lax.rem(ss, 2)
        start = jnp.where(role < 2, tt * 768 + xx * 384, tt * 384)
        return ref.at[pl.ds(pl.multiple_of(zz * 96 + yy * 48, 16), 48), pl.ds(pl.multiple_of(start, 128), 384)]

    @pl.when(role >= 0)
    def _():
        def arrive(i, carry):
            @pl.when(involved(i))
            def _():
                reg = own_region(mbuf, i)
                pltpu.make_async_copy(mb.at[0], reg, m_r.at[i]).wait()
            return carry
        @pl.when(role >= 2)
        def _():
            mbuf[:, 768:1536] = jnp.zeros((mbuf.shape[0], 768), BF16)
        lax.fori_loop(0, 32, arrive, 0)
        newton_schulz(role, mbuf, dbuf, q_hi, q_lo)
        def leave(i, carry):
            reg = own_region(dbuf, i)
            @pl.when(involved(i) & (i != me))
            def _():
                remote(reg, dpc.at[slot], d_s.at[i], d_r.at[slot], dev(i)).start()
            @pl.when(involved(i) & (i == me))
            def _():
                pltpu.make_async_copy(reg, dpc.at[slot], d_r.at[slot]).start()
            return carry
        lax.fori_loop(0, 32, leave, 0)

    ec = []
    def got(i):
        pltpu.make_async_copy(mb.at[0], dpc.at[i], d_r.at[i]).wait()
    for m in order:
        if m:
            got(m)
            delta_sh[m, r48(y), c384(x)] = dpc[m]
        else:
            got(0)
            got(3)
            cc = lax.broadcasted_iota(jnp.int32, (1, 384), 1)
            lead = (cc < 128) | ((cc >= 256) & (t == jnp.where(cc >= 320, 1, 0)))
            delta_sh[m, r48(y), c384(x)] = jnp.where(lead, dpc[0], dpc[3])
        blk = delta_sh.at[m, r48(y), c384(x)]
        for j in range(1, 4):
            ec.append(go(remote(blk, blk, e_s.at[m, j - 1], e_r.at[m, j - 1], sdev(j))))
    for c in ac + ec:
        c.wait_recv()
    for a, (src, dst) in enumerate(((bo, bo_out), (ig, ig_out))):
        for j in range(4):
            sj = sidx(j)
            blk = src.at[pl.ds(0, 64)]
            if j:
                remote(blk, dst.at[sj, t], t_s.at[a, j, 0], t_r.at[a, j, 0], {"seq": sj}).wait_recv()
            remote(blk, dst.at[sj, 1 - t], t_s.at[a, j, 1], t_r.at[a, j, 1], {"seq": sj, "tp": 1 - t}).wait_recv()
    for c in lc:
        c.wait()
    for c in sends:
        c.wait_send()
    for f in fins:
        f()
    @pl.when(role >= 0)
    def _():
        def done(i, carry):
            @pl.when(involved(i) & (i != me))
            def _():
                remote(own_region(dbuf, i), dpc.at[slot], d_s.at[i], d_r.at[slot], dev(i)).wait_send()
            return carry
        lax.fori_loop(0, 32, done, 0)


def reduce(scale, raw, gs, mom, bo, ig):
    vm = pl.BlockSpec(memory_space=pltpu.VMEM)
    d = raw.shape[1]
    D = pltpu.SemaphoreType.DMA
    V = pltpu.VMEM
    rows = bo.shape[0] // 4
    return pl.pallas_call(
        functools.partial(reduce_kernel, scale),
        out_shape=(
            jax.ShapeDtypeStruct((3, 96, 768), BF16),
            jax.ShapeDtypeStruct((3, 96, 768), BF16),
            jax.ShapeDtypeStruct((4, 2, rows, d), BF16),
            jax.ShapeDtypeStruct((4, 2, rows, d), BF16),
            jax.ShapeDtypeStruct((8, d), F32),
        ),
        in_specs=[vm] * 5, out_specs=(vm,) * 5,
        scratch_shapes=[
            V((3, 384, 768), BF16), V((3, 384, 384), F32), V((3, 384, 384), BF16), V((3, 384, 384), BF16),
            V((3, 4, 48, 384), BF16), V((3, 4, 48, 384), BF16), V((3, 3, 48, 384), BF16), V((3, 3, 48, 384), BF16),
            V((3, 48, 384), BF16), V((384, 1536), BF16), V((384, 1536), BF16), V((4, 48, 384), BF16),
            V((384, 384), BF16), V((384, 384), BF16),
            V((8, d), F32), V((8, d), F32), V((8, d), F32), V((4, 8, d), F32), V((2, 8, d), F32),
            D((3,)), D((3,)), D((3,)), D((3,)), D((3,)), D((3,)), D((3, 3)), D((3, 3)), D((3, 3)), D((3, 3)),
            D((4,)), D((32,)), D((32,)), D((4,)), D((3, 3)), D((3, 3)), D((2, 4, 2)), D((2, 4, 2)), D((6,)), D((6,)), D((2,)),
        ],
        compiler_params=pltpu.CompilerParams(collective_id=1, has_side_effects=True, vmem_limit_bytes=60000 * 1024),
        name="reduce",
    )(raw, gs, mom, bo, ig)


def cols(a, lo, n):
    return a[..., lo : lo + n]


def pack(q, k, v, o, t):
    even = jnp.concatenate([cols(q, 0, 128), cols(k, 0, 128), cols(q, 128, 64), cols(k, 128, 64),
                            cols(v, 0, 128), cols(o, 0, 128), cols(v, 128, 64), cols(o, 128, 64)], axis=-1)
    odd = jnp.concatenate([cols(q, 64, 128), cols(k, 64, 128), cols(k, 0, 64), cols(q, 0, 64),
                           cols(v, 64, 128), cols(o, 64, 128), cols(o, 0, 64), cols(v, 0, 64)], axis=-1)
    return jnp.where(t == 0, even, odd)


def unpack(a, t):
    def two(big, first, second):
        even = jnp.concatenate([cols(a, big, 128), cols(a, first, 64)], -1)
        odd = jnp.concatenate([cols(a, second, 64), cols(a, big, 128)], -1)
        return jnp.where(t == 0, even, odd)
    return two(0, 256, 320), two(128, 320, 256), two(384, 640, 704), two(512, 704, 640)


def body(tokens, lengths, grad_out, qkv_weight, out_weight, up_weight, down_weight, attn_gain, ffn_gain,
         moment_qkv, moment_out, moment_up, moment_down, moment_attn, moment_ffn):
    micro, img_dev, tok_loc, width = tokens.shape
    fsdp = lax.axis_size("fsdp")
    rep = fsdp // 4
    fi, s, t = lax.axis_index("fsdp"), lax.axis_index("seq"), lax.axis_index("tp")
    z, fr = fi // rep, lax.rem(fi, rep)
    full = tok_loc * lax.axis_size("seq")
    scale = (micro * img_dev * fsdp * full) ** (-0.5)
    groups = [[a * rep + b for b in range(rep)] for a in range(4)]

    def packed(qkv, out, up, down):
        return jnp.stack([pack(qkv[0], qkv[1], qkv[2], out.T, t), up, down.T])

    def widen(a, axis):
        return a if rep == 1 else lax.all_gather(a, "fsdp", axis=axis, tiled=True, axis_index_groups=groups)

    wsh = widen(packed(qkv_weight, out_weight, up_weight, down_weight).astype(BF16), 1)
    mom = widen(packed(moment_qkv, moment_out, moment_up, moment_down), 1)
    gains = widen(jnp.stack([attn_gain, ffn_gain]).astype(BF16), 1)
    gsh = lax.dynamic_update_slice(jnp.zeros((16, width), BF16), gains, (0, z * gains.shape[1]))

    w, gains, x, g = gather(tokens, grad_out, wsh, gsh)
    length = lax.dynamic_slice(lengths, (s, t), (1, 1)).reshape(1)
    bo, ig, raw, gsum = compute(length, x, g, w, gains)
    if rep > 1:
        rgroups = groups
        raw = lax.psum(raw.astype(F32), "fsdp", axis_index_groups=rgroups).astype(BF16)
        gsum = lax.psum(gsum, "fsdp", axis_index_groups=rgroups)
    grad, delta, bo, ig, gsum = reduce(scale, raw, gsum, mom, bo, ig)

    def narrow(a):
        n = qkv_weight.shape[1]
        return a if rep == 1 else lax.dynamic_slice_in_dim(a, fr * n, n, axis=1)

    grad = narrow(grad).astype(F32)
    delta = narrow(delta).astype(F32)
    def parts(a):
        q, k, v, o = unpack(a[0], t)
        return jnp.stack([q, k, v]), o.T, a[1], a[2].T
    gq, go, gu, gd = parts(grad)
    dq, do, du, dd = parts(delta)
    n = attn_gain.shape[0]
    ga, gf = lax.dynamic_slice(gsum, (0, fi * n), (2, n))
    mq, mo, mu, md = 0.5 * moment_qkv + gq, 0.5 * moment_out + go, 0.5 * moment_up + gu, 0.5 * moment_down + gd
    ma, mf = 0.5 * moment_attn + ga, 0.5 * moment_ffn + gf
    return (bo, ig.astype(F32), gq, go, gu, gd, ga, gf,
            qkv_weight - dq, out_weight - do, up_weight - du, down_weight - dd,
            attn_gain - 0.3 * ma, ffn_gain - 0.3 * mf, mq, mo, mu, md, ma, mf)


def solution(mesh):
    weights = (P(None, "fsdp", "tp"), P("tp", "fsdp"), P("fsdp", "tp"), P("tp", "fsdp"), P("fsdp"), P("fsdp"))
    rows = P(None, "fsdp", "seq", None)
    return jax.shard_map(body, mesh=mesh, in_specs=(rows, P(None, "fsdp"), rows) + weights + weights,
                         out_specs=(rows, rows) + weights + weights + weights, check_vma=False)
```

time: 950 us -> 145 us (0.15)
  waiting for transfers between devices: 413 us -> 0 us
  blocking collectives: 267 us -> 0 us
  Pallas kernels: 0 us -> 118 us
  matrix products: 104 us -> 0 us
  local copies, waits for them, and re-layouts: 63.6 us -> 9.8 us
  other arithmetic: 49.8 us -> 14.8 us
  loops' own time: 23.4 us -> 0 us
  between operations: 18.6 us -> 1.01 us
    reduce_scatter x10 -> x0, waiting for transfers between devices: 193 us -> none  [the longest x4 79 us: body(): lax.psum_scatter(key_part, 'seq', scatter_dimension=1, tiled=True)]
    all_gather x15 -> x0, blocking collectives: 192 us -> none  [the longest x1 43.8 us: body(): lax.all_gather(new_moment_qkv, 'fsdp', axis=1, tiled=True)]
    psum x5 -> x0, waiting for transfers between devices: 141 us -> none  [the longest x1 57.8 us: body(): lax.psum(shortened(mine), ('fsdp', 'tp'))]
    pallas_call x0 -> x3, Pallas kernels: none -> 118 us  [the longest x1 72.7 us: reduce(): pl.pallas_call(functools.partial(reduce_kernel, scale), out_shape=(jax.Sh...]
    dot_general x83 -> x0, matrix products: 103 us -> none  [the longest x4 15.2 us: body(): jnp.einsum('ihqk,ikhe->iqhe', back_scores, keys_h, preferred_element_type...]
    unnamed x2 -> x0, blocking collectives: 65 us -> none
    all_gather x5 -> x0, waiting for transfers between devices: 45.8 us -> none  [the longest x1 31.8 us: body(): lax.all_gather(new_moment_down, 'fsdp', axis=1, tiled=True)]
    unnamed x24 -> x0, waiting for transfers between devices: 33 us -> none
  transfers between devices with their start and end apart: 22 -> 0, of which waited for: 17 -> 0; matrix products, arithmetic and copies ran while one was open for 14% -> 0% of each run, Pallas kernels for 0% -> 0%
where the time goes in v1:
time: 145 us; the launch traced here: 143 us
  Pallas kernels  118 us (81%)
  other arithmetic  14.8 us (10%)
  local copies, waits for them, and re-layouts  9.8 us (7%)
    pallas_call x1, Pallas kernels, reduce(): pl.pallas_call(functools.partial(reduce_kernel, scale), out_shape=(jax.Sh...  72.7 us
    pallas_call x1, Pallas kernels, gather(): pl.pallas_call(gather_kernel, out_shape=(jax.ShapeDtypeStruct((3, d, 4 *...  31.8 us
    pallas_call x1, Pallas kernels, compute(): pl.pallas_call(compute_kernel, out_shape=(jax.ShapeDtypeStruct((rows, d),...  13.1 us
    unnamed x36, local copies, waits for them, and re-layouts  4.69 us
    another operation x4, other arithmetic, packed(): return jnp.stack([pack(qkv[0], qkv[1], qkv[2], out.T, t), up, down.T])  3.81 us

profile of v1, /device:TPU:0, one launch (start us, length us, event | category | flops | bytes accessed | tf_op | source)
XLA Modules:
  0.0 143.2 jit_solution(5343083419334229888)
XLA Ops:
  0.7 1.0 slice_bitcast_fusion.9
  1.8 1.0 copy.35
  3.2 1.0 convert_bitcast_fusion
  4.2 1.0 convert_bitcast_fusion.1
  5.2 0.8 pad_maximum_fusion.1.wsh
  6.1 0.3 dynamic_update_slice.3.gsh
  6.4 0.6 copy-done.9
  7.0 31.8 %gather.1 = (bf16[3,384,1536]{2,1,0:T(8,128)(2,1)}, bf16[4,16,384]{2,1,0:T(8,128)(2,1)}, bf16[256,384]{1,0:T(8,128)(2,1)}, bf16[256,384]{1,0:T(8,128)(2,1)}) custom-call(bf16[4,2,64,384]{3,2,1,0:T(8,128)(2,1)} %tok.1, bf16[4,2,64,384]{3,2,1,0:T(8,128)(2,1)} %go.1, bf16[3,96,768]{2,1,0:T(8,128)(2,1)} %pad_maximum_fusion.1.wsh, bf16[16,384]{1,0:T(8,128)(2,1)} %copy-done.9), custom_call_target="tpu_custom_call" | custom-call | tf_op jit(solution)/shard_map/gather/pallas_call | solution.py:112
  38.8 0.6 dynamic_slice.6
  39.4 13.1 %image.1 = (bf16[256,384]{1,0:T(8,128)(2,1)}, bf16[256,384]{1,0:T(8,128)(2,1)}, bf16[3,384,1536]{2,1,0:T(8,128)(2,1)}, f32[8,384]{1,0:T(8,128)}) custom-call(s32[1]{0:T(128)} %bitcast.len_ref, bf16[256,384]{1,0:T(8,128)(2,1)} %get-tuple-element.33.x_ref, bf16[256,384]{1,0:T(8,128)(2,1)} %get-tuple-element.34.g_ref, ...), custom_call_target="tpu_custom_call" | custom-call | tf_op jit(solution)/shard_map/image/pallas_call | solution.py:273
  53.2 1.0 pad_maximum_fusion.mom
  54.1 72.7 %reduce.1 = (bf16[3,96,768]{2,1,0:T(8,128)(2,1)}, bf16[3,96,768]{2,1,0:T(8,128)(2,1)}, bf16[4,2,64,384]{3,2,1,0:T(8,128)(2,1)}, bf16[4,2,64,384]{3,2,1,0:T(8,128)(2,1)}, f32[8,384]{1,0:T(8,128)}) custom-call(bf16[3,384,1536]{2,1,0:T(8,128)(2,1)} %get-tuple-element.37.raw, f32[8,384]{1,0:T(8,128)} %get-tuple-element.38.gs, ...), custom_call_target="tpu_custom_call" | custom-call | tf_op jit(solution)/shard_map/reduce/pallas_call | solution.py:639
  126.8 1.1 convert_element_type.13
  128.2 0.7 copy.40
  128.9 0.1 maximum_select_fusion.4
  129.1 0.8 maximum_subtract_fusion
  129.9 1.1 convert_element_type.12
  131.0 0.7 fusion.8
  131.8 0.7 fusion.9
  132.5 0.7 copy.39
  133.2 0.7 copy.41
  134.0 1.2 maximum_select_fusion
  135.2 1.0 maximum_select_fusion.2
  136.1 0.9 multiply_add_fusion.2
  137.0 0.8 multiply_add_fusion.1
  137.9 0.8 multiply_add_fusion
  138.7 0.7 fusion
  139.5 0.7 fusion.1
  140.2 0.9 convert_element_type.11
  141.1 0.8 constant_dynamic-slice_fusion
  141.9 0.5 multiply_subtract_fusion
  142.5 0.7 copy.44
  (55 shorter events, 1.5 us)
Async XLA Ops:
  0.7 5.4 %copy-start.11 = (f32[96]{0:T(128)S(1)}, f32[96]{0:T(128)}, u32[]{:S(2)}) copy-start(f32[96]{0:T(128)} %param.22) | copy-start | bytes 1156
  0.7 5.4 %copy-start.10 = (f32[96]{0:T(128)S(1)}, f32[96]{0:T(128)}, u32[]{:S(2)}) copy-start(f32[96]{0:T(128)} %param.23) | copy-start | bytes 1156
  0.7 38.1 %copy-start.14 = (s32[4,2]{0,1:T(2,128)S(1)}, s32[4,2]{0,1:T(2,128)}, u32[]{:S(2)}) copy-start(s32[4,2]{0,1:T(2,128)} %param.16) | copy-start | bytes 100
  3.2 49.3 %copy-start.4 = (f32[3,96,192]{2,1,0:T(8,128)S(1)}, f32[3,96,192]{2,1,0:T(8,128)}, u32[]{:S(2)}) copy-start(f32[3,96,192]{2,1,0:T(8,128)} %param.24) | copy-start | bytes 663556
  6.0 46.6 %copy-start.8 = (f32[192,96]{1,0:T(8,128)S(1)}, f32[192,96]{1,0:T(8,128)}, u32[]{:S(2)}) copy-start(f32[192,96]{1,0:T(8,128)} %param.25) | copy-start | bytes 221188
  6.4 0.6 copy-start.9
  39.4 13.7 %copy-start.2 = (f32[96,768]{1,0:T(8,128)S(1)}, f32[96,768]{1,0:T(8,128)}, u32[]{:S(2)}) copy-start(f32[96,768]{1,0:T(8,128)} %param.26) | copy-start | bytes 884740
  39.4 13.8 %copy-start.3 = (f32[768,96]{0,1:T(8,128)S(1)}, f32[768,96]{0,1:T(8,128)}, u32[]{:S(2)}) copy-start(f32[768,96]{0,1:T(8,128)} %param.27) | copy-start | bytes 884740
  54.1 75.0 %copy-start.5 = (f32[3,96,192]{2,1,0:T(8,128)S(1)}, f32[3,96,192]{2,1,0:T(8,128)}, u32[]{:S(2)}) copy-start(f32[3,96,192]{2,1,0:T(8,128)} %param.18) | copy-start | bytes 663556
  131.0 7.7 %copy-start = (f32[768,96]{0,1:T(8,128)S(1)}, f32[768,96]{0,1:T(8,128)}, u32[]{:S(2)}) copy-start(f32[768,96]{0,1:T(8,128)} %param.21) | copy-start | bytes 884740
  131.0 8.4 %copy-start.1 = (f32[96,768]{1,0:T(8,128)S(1)}, f32[96,768]{1,0:T(8,128)}, u32[]{:S(2)}) copy-start(f32[96,768]{1,0:T(8,128)} %param.20) | copy-start | bytes 884740
  134.0 6.2 %copy-start.7 = (bf16[4,2,64,384]{3,2,1,0:T(8,128)(2,1)S(1)}, bf16[4,2,64,384]{3,2,1,0:T(8,128)(2,1)}, u32[]{:S(2)}) copy-start(bf16[4,2,64,384]{3,2,1,0:T(8,128)(2,1)} %get-tuple-element.42) | copy-start | bytes 1179652
  134.0 7.9 %copy-start.12 = (f32[96]{0:T(128)S(1)}, f32[96]{0:T(128)}, u32[]{:S(2)}) copy-start(f32[96]{0:T(128)} %param.29) | copy-start | bytes 1156
  134.0 7.9 %copy-start.13 = (f32[96]{0:T(128)S(1)}, f32[96]{0:T(128)}, u32[]{:S(2)}) copy-start(f32[96]{0:T(128)} %param.28) | copy-start | bytes 1156
  134.0 8.5 %copy-start.6 = (bf16[4,2,64,384]{3,2,1,0:T(8,128)(2,1)S(1)}, bf16[4,2,64,384]{3,2,1,0:T(8,128)(2,1)}, u32[]{:S(2)}) copy-start(bf16[4,2,64,384]{3,2,1,0:T(8,128)(2,1)} %get-tuple-element.183) | copy-start | bytes 1179652
